TPU v7x, 128 devices: a whole 4x4x4 slice. The times are simulated.
128 devices in a mesh: dp: 32 (over x, z, core), tp: 4 (over y).
Axes of the slice: x: 4, y: 4, z: 4, core: 2. Of those that a mesh axis runs over, the one named last changes fastest.
Arguments:
- hidden_in: bfloat16 [2048, 3584], P(('dp', 'tp')), may hold values from -6 to 6
- query_latent: bfloat16 [2048, 64, 512], P(('dp', 'tp')), may hold values from -348 to 347
- query_rope: bfloat16 [2048, 4096], P(('dp', 'tp')), may hold values from -348 to 347
- cache_latent: bfloat16 [2048, 128, 512], P(('dp', 'tp')), may hold values from -6 to 6
- cache_rope: bfloat16 [2048, 64, 128], P(('dp', 'tp')), may hold values from -6 to 6
- lengths: int32 [2048], P(('dp', 'tp')), may hold values from 16 to 128
- value_up: bfloat16 [512, 4096], P(None, 'tp'), may hold values from -1 to 1
- out_proj: bfloat16 [4096, 3584], P('tp'), may hold values from -0.09375 to 0.09375
- norm_gain: float32 [3584], replicated, may hold values from 0.1 to 1.9
- expert_gate: bfloat16 [128, 3584, 1024], P(('dp', 'tp')), may hold values from -0.09375 to 0.09375
- expert_down: bfloat16 [128, 1024, 3584], P(('dp', 'tp')), may hold values from -0.1875 to 0.1875
- expert_ids: int32 [2048, 8], P(('dp', 'tp')), may hold values from 0 to 127, all different within a row; in each aligned block of 16 rows (0 to 15, 16 to 31, ...) at most 2 rows name the same one
- affinity: float32 [2048, 8], P(('dp', 'tp')), may hold values from 0.05 to 1
Outputs:
- layer_out: bfloat16 [2048, 3584], P(('dp', 'tp'))
Inputs may be any that keep to these rules, and one draw needn't show every extreme that they name: `expert_ids`: in each aligned block of 16 rows (the rows of one device) no expert is named by more than 2 rows.
All inputs are finite; a program needn't handle non-finite values.
Results may differ from a plain program's by a relative error of at most 0.0081.
Values may be sent and summed in bfloat16 or wider, within the bound.
A program may use at most 128 MiB of HBM per device.

v0:
```python
import jax
import jax.numpy as jnp
from jax import lax
from jax.sharding import PartitionSpec as P

score_scale = 192.0 ** (-0.5)
norm_eps = 1e-06
route_scale = 2.5


def in_blocks(shard, dim, peers):
    before, after = (shard.shape[:dim], shard.shape[dim + 1 :])
    return jnp.moveaxis(shard.reshape(*before, peers, -1, *after), dim, 0)


def sum_at_owner(shard, axis, dim):
    peers = lax.axis_size(axis)
    parts = lax.all_to_all(in_blocks(shard, dim, peers), axis, 0, 0, tiled=True)
    return jnp.sum(parts.astype(jnp.float32), axis=0)


def attend(query_latent, query_rope, cache_latent, cache_rope, lengths):
    token_count, head_count, latent_width = query_latent.shape
    rope_width = cache_rope.shape[1]
    context = cache_latent.shape[1]
    query_rot = query_rope.reshape(token_count, head_count, rope_width)
    scores = jnp.einsum(
        "thl,tpl->thp", query_latent, cache_latent, preferred_element_type=jnp.float32
    )
    scores = scores + jnp.einsum(
        "thr,trp->thp", query_rot, cache_rope, preferred_element_type=jnp.float32
    )
    scores = scores * score_scale
    position = lax.broadcasted_iota(jnp.int32, (token_count, 1, context), 2)
    scores = jnp.where(position < lengths[:, None, None], scores, -jnp.inf)
    row_max = jnp.max(scores, axis=2, keepdims=True)
    raised = jnp.exp(scores - row_max)
    attn_weights = (raised / jnp.sum(raised, axis=2, keepdims=True)).astype(jnp.bfloat16)
    latent_out = jnp.einsum(
        "thp,tpl->thl", attn_weights, cache_latent, preferred_element_type=jnp.float32
    )
    return latent_out.astype(jnp.bfloat16)


def per_device(
    hidden_in,
    query_latent,
    query_rope,
    cache_latent,
    cache_rope,
    lengths,
    value_up,
    out_proj,
    norm_gain,
    expert_gate,
    expert_down,
    expert_ids,
    affinity,
):
    latent_out = attend(query_latent, query_rope, cache_latent, cache_rope, lengths)
    group_size = lax.axis_size("tp")
    local_heads = latent_out.shape[1] // group_size
    by_heads = lax.all_to_all(latent_out, "tp", split_axis=1, concat_axis=0, tiled=True)
    head_width = value_up.shape[1] // local_heads
    up_table = value_up.reshape(value_up.shape[0], local_heads, head_width)
    per_head = jnp.einsum(
        "thl,lhv->thv", by_heads, up_table, preferred_element_type=jnp.float32
    ).astype(jnp.bfloat16)
    attn_sum = sum_at_owner(
        jnp.dot(
            per_head.reshape(hidden_in.shape[0] * lax.axis_size("tp"), local_heads * head_width),
            out_proj,
            preferred_element_type=jnp.float32,
        ).astype(jnp.bfloat16),
        "tp",
        0,
    )
    hidden = (hidden_in.astype(jnp.float32) + attn_sum).astype(jnp.bfloat16)
    wide_hidden = hidden.astype(jnp.float32)
    inv_norm = lax.rsqrt(jnp.mean(wide_hidden * wide_hidden, axis=1, keepdims=True) + norm_eps)
    normed = (wide_hidden * inv_norm * norm_gain).astype(jnp.bfloat16)
    tok_rows, top_count = expert_ids.shape
    width = normed.shape[1]
    experts = expert_gate.shape[0] * lax.axis_size("dp") * lax.axis_size("tp")
    capacity = max(2, -(-(tok_rows * top_count) // experts))
    flat_ids = expert_ids.reshape(-1)
    expert_iota = lax.broadcasted_iota(jnp.int32, (1, experts), 1)
    one_hot = (flat_ids[:, None] == expert_iota).astype(jnp.int32)
    earlier = jnp.cumsum(one_hot, axis=0) - one_hot
    slot_index = jnp.sum(earlier * one_hot, axis=1)
    target = flat_ids * capacity + slot_index
    owner_row = jnp.arange(tok_rows * top_count, dtype=jnp.int32) // top_count
    source_row = jnp.full((experts * capacity,), tok_rows, jnp.int32).at[target].set(owner_row)
    padded = jnp.concatenate([normed, jnp.zeros((1, width), jnp.bfloat16)], axis=0)
    outgoing = padded[source_row].reshape(experts, capacity, width)
    gate_local = expert_gate[0]
    down_local = expert_down[0]
    slot_rows = lax.all_to_all(outgoing, ("dp", "tp"), split_axis=0, concat_axis=0, tiled=True)
    lead_shape = slot_rows.shape[:-1]
    flat_rows = slot_rows.reshape(-1, width)
    inner_act = jax.nn.silu(
        jnp.dot(flat_rows, gate_local, preferred_element_type=jnp.float32)
    ).astype(jnp.bfloat16)
    answer = jnp.dot(inner_act, down_local, preferred_element_type=jnp.float32).astype(jnp.bfloat16)
    answered = answer.reshape(lead_shape + (width,))
    returned = lax.all_to_all(answered, ("dp", "tp"), split_axis=0, concat_axis=0, tiled=True)
    returned = returned.reshape(experts * capacity, width)
    picked = returned[target].reshape(tok_rows, top_count, width).astype(jnp.float32)
    route_weight = route_scale * affinity / jnp.sum(affinity, axis=1, keepdims=True)
    moe_sum = jnp.sum(picked * route_weight[:, :, None], axis=1)
    return (wide_hidden + moe_sum).astype(jnp.bfloat16)


def solution(mesh):
    return jax.shard_map(
        per_device,
        mesh=mesh,
        in_specs=(
            P(("dp", "tp"), None),
            P(("dp", "tp"), None, None),
            P(("dp", "tp"), None),
            P(("dp", "tp"), None, None),
            P(("dp", "tp"), None, None),
            P(("dp", "tp")),
            P(None, "tp"),
            P("tp", None),
            P(),
            P(("dp", "tp"), None, None),
            P(("dp", "tp"), None, None),
            P(("dp", "tp"), None),
            P(("dp", "tp"), None),
        ),
        out_specs=P(("dp", "tp"), None),
        check_vma=False,
    )
```

profile of v0, /device:TPU:1, one launch (start us, length us, event | category | flops | bytes accessed | tf_op | source)
XLA Modules:
  0.0 159.0 jit_solution(15531151931945262616)
XLA Ops:
  0.0 0.0 copy-start
  0.0 1.3 reshape.88
  1.3 0.7 iota_compare_fusion.1
  2.1 1.2 fusion.31
  3.2 0.0 copy-done
  3.2 2.1 %fusion.12 = f32[16,64,128]{2,1,0:T(8,128)S(1)} fusion(f32[16,64,128]{2,1,0:T(8,128)S(1)} %fusion.31, bf16[16,64,512]{2,1,0:T(8,128)(2,1)} %param.14, bf16[16,128,512]{2,1,0:T(8,128)(2,1)S(1)} %copy-done, pred[16,128]{1,0:T(8,128)(4,1)S(1)} %iota_compare_fusion.1), kind=kOutput, calls=%fused_computation.17 | convolution fusion | flops 134610944 | bytes 4196352 | tf_op jit(solution)/shard_map/thl,tpl->thp/dot_general | solution.py:27
  5.3 0.3 fusion.30
  5.7 3.0 %convolution_convert_fusion.1 = bf16[16,64,512]{2,1,0:T(8,128)(2,1)} fusion(bf16[16,128,512]{2,1,0:T(8,128)(2,1)S(1)} %copy-done, f32[16,64]{1,0:T(8,128)S(1)} %fusion.30, f32[16,64,128]{2,1,0:T(8,128)S(1)} %fusion.12), kind=kOutput, calls=%fused_computation.12 | convolution fusion | flops 135136384 | bytes 3674112 | tf_op jit(solution)/shard_map/thp,tpl->thl/dot_general | solution.py:39
  8.6 2.8 %copy.25 = bf16[16,64,512]{2,0,1:T(8,128)(2,1)} copy(bf16[16,64,512]{2,1,0:T(8,128)(2,1)} %convolution_convert_fusion.1) | data formatting | bytes 2097152 | tf_op jit(solution)/shard_map/convert_element_type | solution.py:42
  11.4 0.0 copy-start.3
  11.4 5.1 %all-to-all-start = ((bf16[16,64,512]{2,0,1:T(8,128)(2,1)}), bf16[16,64,512]{2,0,1:T(8,128)(2,1)S(1)}, u32[]{:S(2)}, u32[]{:S(2)}) async-start(bf16[16,64,512]{2,0,1:T(8,128)(2,1)} %copy.25), calls=%async_computation | async-start | bytes 2097152 | tf_op jit(solution)/shard_map/all_to_all | solution.py:63
  16.6 2.3 %copy.27 = bf16[512,1024]{0,1:T(8,128)(2,1)} copy(bf16[512,1024]{1,0:T(8,128)(2,1)} %param.19) | data formatting | bytes 2097152 | tf_op args[6]
  18.8 0.0 copy-done.3
  18.8 0.1 copy.30
  18.9 0.1 eq.15
  19.0 0.1 copy.29
  19.1 0.1 mul.71
  19.2 0.1 fusion.24
  19.3 0.2 reduce_window_sum.11
  19.4 0.2 select_reduce_fusion
  19.6 11.2 %all-to-all-done = bf16[16,64,512]{2,0,1:T(8,128)(2,1)S(1)} async-done(((bf16[16,64,512]{2,0,1:T(8,128)(2,1)}), bf16[16,64,512]{2,0,1:T(8,128)(2,1)S(1)}, u32[]{:S(2)}, u32[]{:S(2)}) %all-to-all-start) | async-done | bytes 1048608 | tf_op jit(solution)/shard_map/all_to_all | solution.py:63
  30.8 0.0 copy-start.1
  30.8 0.1 copy.26
  30.9 1.1 copy-done.1
  32.0 0.4 fusion.13
  32.4 0.2 copy.28
  32.6 0.2 reshape.90
  32.8 0.0 copy-start.2
  32.8 0.0 copy-start.5
  32.8 5.3 %convolution_convert_fusion = bf16[64,3584]{1,0:T(8,128)(2,1)} fusion(bf16[64,1024]{1,0:T(8,128)(2,1)S(1)} %reshape.90, bf16[1024,3584]{1,0:T(8,128)(2,1)} %param.20), kind=kOutput, calls=%fused_computation.9 | convolution fusion | flops 469991424 | bytes 7929856 | tf_op jit(solution)/shard_map/dot_general | solution.py:70
  38.1 3.5 %all-to-all-start.1 = ((bf16[4,16,3584]{2,1,0:T(8,128)(2,1)}), bf16[4,16,3584]{2,1,0:T(8,128)(2,1)S(1)}, u32[]{:S(2)}, u32[]{:S(2)}) async-start(bf16[4,16,3584]{2,1,0:T(8,128)(2,1)} %bitcast.5), calls=%async_computation.1 | async-start | bytes 917504 | tf_op jit(solution)/shard_map/all_to_all | solution.py:18
  41.6 1.0 scatter_custom_fusion
  42.6 5.7 %all-to-all-done.1 = bf16[4,16,3584]{2,1,0:T(8,128)(2,1)S(1)} async-done(((bf16[4,16,3584]{2,1,0:T(8,128)(2,1)}), bf16[4,16,3584]{2,1,0:T(8,128)(2,1)S(1)}, u32[]{:S(2)}, u32[]{:S(2)}) %all-to-all-start.1) | async-done | bytes 458784 | tf_op jit(solution)/shard_map/all_to_all | solution.py:18
  48.3 0.1 convert_reduce_fusion
  48.4 0.0 copy-done.2
  48.4 0.2 fusion.20
  48.6 0.0 copy-done.5
  48.6 0.1 fusion.22
  48.7 2.9 %gather_fusion = bf16[256,3584]{1,0:T(8,128)(2,1)} fusion(bf16[17,3584]{1,0:T(8,128)(2,1)S(1)} %concatenate.3, s32[1024]{0:T(1024)S(1)} %pad_clamp_fusion.1), kind=kCustom, calls=%fused_computation | custom fusion | bytes 3671040 | tf_op jit(solution)/shard_map/gather | solution.py:95
  51.6 4.8 %reshape.92 = bf16[128,2,3584]{2,1,0:T(2,128)(2,1)} reshape(bf16[256,3584]{1,0:T(8,128)(2,1)} %gather_fusion) | data formatting | bytes 3670016 | tf_op jit(solution)/shard_map/reshape | solution.py:95
  56.4 39.2 %all_to_all.33 = bf16[128,2,3584]{2,1,0:T(2,128)(2,1)} all-to-all(bf16[128,2,3584]{2,1,0:T(2,128)(2,1)} %reshape.92), channel_id=1, replica_groups=mesh['dp'=32,'tp'=4] {'dp','tp'}, dimensions={0} | all-to-all | bytes 3670016 | tf_op jit(solution)/shard_map/all_to_all | solution.py:98
  95.7 5.0 %reshape.93 = bf16[256,3584]{1,0:T(8,128)(2,1)} reshape(bf16[128,2,3584]{2,1,0:T(2,128)(2,1)} %all_to_all.33) | data formatting | bytes 3670016 | tf_op jit(solution)/shard_map/reshape | solution.py:100
  100.6 10.9 %fusion.5 = bf16[256,3584]{1,0:T(8,128)(2,1)} fusion(bf16[1,1024,3584]{2,1,0:T(8,128)(2,1)} %param.23, bf16[256,3584]{1,0:T(8,128)(2,1)} %reshape.93, bf16[1,3584,1024]{2,1,0:T(8,128)(2,1)} %param.22), kind=kOutput, calls=%fused_computation.8 | convolution fusion | flops 3760324608 | bytes 18350080 | tf_op jit(solution)/shard_map/dot_general | solution.py:104
  111.5 4.8 %reshape.94 = bf16[128,2,3584]{2,1,0:T(2,128)(2,1)} reshape(bf16[256,3584]{1,0:T(8,128)(2,1)} %fusion.5) | data formatting | bytes 3670016 | tf_op jit(solution)/shard_map/reshape | solution.py:105
  116.3 0.0 copy-start.4
  116.3 4.8 %all-to-all-start.3 = ((bf16[128,2,3584]{2,1,0:T(2,128)(2,1)}), bf16[128,2,3584]{2,1,0:T(2,128)(2,1)}, u32[]{:S(2)}, u32[]{:S(2)}) async-start(bf16[128,2,3584]{2,1,0:T(2,128)(2,1)} %reshape.94), calls=%async_computation.3 | async-start | bytes 3670016 | tf_op jit(solution)/shard_map/all_to_all | solution.py:106
  121.0 0.0 copy-done.4
  121.1 0.1 copy.31
  121.2 27.8 %all-to-all-done.3 = bf16[128,2,3584]{2,1,0:T(2,128)(2,1)} async-done(((bf16[128,2,3584]{2,1,0:T(2,128)(2,1)}), bf16[128,2,3584]{2,1,0:T(2,128)(2,1)}, u32[]{:S(2)}, u32[]{:S(2)}) %all-to-all-start.3) | async-done | bytes 1835040 | tf_op jit(solution)/shard_map/all_to_all | solution.py:106
  149.0 4.9 %reshape.95 = bf16[256,3584]{1,0:T(8,128)(2,1)} reshape(bf16[128,2,3584]{2,1,0:T(2,128)(2,1)} %all-to-all-done.3) | data formatting | bytes 3670016 | tf_op jit(solution)/shard_map/reshape | solution.py:107
  153.9 3.8 %gather_fusion.1 = bf16[128,3584]{1,0:T(8,128)(2,1)S(1)} fusion(bf16[256,3584]{1,0:T(8,128)(2,1)} %reshape.95, s32[1024]{0:T(1024)S(1)} %pad_clamp_fusion), kind=kCustom, calls=%fused_computation.1 | custom fusion | bytes 1835520 | tf_op jit(solution)/shard_map/gather | solution.py:108
  157.7 0.7 fusion.8
  158.3 0.7 fusion.23
  (10 shorter events, 0.1 us)
Async XLA Ops:
  0.0 3.2 %copy-start = (bf16[16,128,512]{2,1,0:T(8,128)(2,1)S(1)}, bf16[16,128,512]{2,1,0:T(8,128)(2,1)}, u32[]{:S(2)}) copy-start(bf16[16,128,512]{2,1,0:T(8,128)(2,1)} %param.16) | copy-start | bytes 6291460
  11.4 7.4 %copy-start.3 = (s32[16,8]{0,1:T(8,128)S(1)}, s32[16,8]{0,1:T(8,128)}, u32[]{:S(2)}) copy-start(s32[16,8]{0,1:T(8,128)} %param.24) | copy-start | bytes 1540
  11.4 19.4 %all-to-all-start = ((bf16[16,64,512]{2,0,1:T(8,128)(2,1)}), bf16[16,64,512]{2,0,1:T(8,128)(2,1)S(1)}, u32[]{:S(2)}, u32[]{:S(2)}) async-start(bf16[16,64,512]{2,0,1:T(8,128)(2,1)} %copy.25), calls=%async_computation | async-start | bytes 2097152 | tf_op jit(solution)/shard_map/all_to_all | solution.py:63
  30.8 1.2 copy-start.1
  32.8 15.6 %copy-start.2 = (bf16[16,3584]{1,0:T(8,128)(2,1)S(1)}, bf16[16,3584]{1,0:T(8,128)(2,1)}, u32[]{:S(2)}) copy-start(bf16[16,3584]{1,0:T(8,128)(2,1)} %param.13) | copy-start | bytes 344068
  32.8 15.7 %copy-start.5 = (f32[3584]{0:T(1024)S(1)}, f32[3584]{0:T(1024)}, u32[]{:S(2)}) copy-start(f32[3584]{0:T(1024)} %param.21) | copy-start | bytes 43012
  38.1 10.2 %all-to-all-start.1 = ((bf16[4,16,3584]{2,1,0:T(8,128)(2,1)}), bf16[4,16,3584]{2,1,0:T(8,128)(2,1)S(1)}, u32[]{:S(2)}, u32[]{:S(2)}) async-start(bf16[4,16,3584]{2,1,0:T(8,128)(2,1)} %bitcast.5), calls=%async_computation.1 | async-start | bytes 917504 | tf_op jit(solution)/shard_map/all_to_all | solution.py:18
  116.3 4.8 %copy-start.4 = (f32[16,8]{0,1:T(8,128)S(1)}, f32[16,8]{0,1:T(8,128)}, u32[]{:S(2)}) copy-start(f32[16,8]{0,1:T(8,128)} %param.25) | copy-start | bytes 1540
  116.3 32.7 %all-to-all-start.3 = ((bf16[128,2,3584]{2,1,0:T(2,128)(2,1)}), bf16[128,2,3584]{2,1,0:T(2,128)(2,1)}, u32[]{:S(2)}, u32[]{:S(2)}) async-start(bf16[128,2,3584]{2,1,0:T(2,128)(2,1)} %reshape.94), calls=%async_computation.3 | async-start | bytes 3670016 | tf_op jit(solution)/shard_map/all_to_all | solution.py:106
where the time goes:
time: 160 us; the launch traced here: 159 us
  waiting for transfers between devices  44.7 us (28%)
  blocking collectives  39.2 us (25%)
  local copies, waits for them, and re-layouts  35.5 us (22%)
  matrix products  22.8 us (14%)
  starting transfers between devices  13.4 us (8%)
  other arithmetic  3.25 us (2%)
    all_to_all x1, blocking collectives, per_device(): lax.all_to_all(outgoing, ('dp', 'tp'), split_axis=0, concat_axis=0, tiled...  39.2 us
    all_to_all x1, waiting for transfers between devices, per_device(): lax.all_to_all(answered, ('dp', 'tp'), split_axis=0, concat_axis=0, tiled...  27.8 us
    all_to_all x1, waiting for transfers between devices, per_device(): lax.all_to_all(latent_out, 'tp', split_axis=1, concat_axis=0, tiled=True)  11.2 us
    dot_general x1, matrix products, per_device(): jnp.dot(inner_act, down_local, preferred_element_type=jnp.float32)  10.9 us
    all_to_all x1, waiting for transfers between devices, sum_at_owner(): parts = lax.all_to_all(in_blocks(shard, dim, peers), axis, 0, 0, tiled=True)  5.71 us
    dot_general x1, matrix products, per_device(): jnp.dot(per_head.reshape(hidden_in.shape[0] * lax.axis_size('tp'), local_...  5.27 us
    all_to_all x1, starting transfers between devices, per_device(): lax.all_to_all(latent_out, 'tp', split_axis=1, concat_axis=0, tiled=True)  5.14 us
    reshape x1, local copies, waits for them, and re-layouts, per_device(): flat_rows = slot_rows.reshape(-1, width)  4.95 us
  transfers between devices with their start and end apart: 3, of which 3 were waited for; matrix products, arithmetic and copies ran while one was open for 3% of the time, Pallas kernels for 0%

commit v1 on v0

--- a/solution.py
+++ b/solution.py
@@ -60,7 +60,11 @@
     latent_out = attend(query_latent, query_rope, cache_latent, cache_rope, lengths)
     group_size = lax.axis_size("tp")
     local_heads = latent_out.shape[1] // group_size
-    by_heads = lax.all_to_all(latent_out, "tp", split_axis=1, concat_axis=0, tiled=True)
+    piece_now = lax.axis_size("tp")
+    part_next = jnp.split(latent_out, piece_now, 1)
+    w2 = jnp.stack(part_next)
+    k_now = lax.all_to_all(w2, "tp", split_axis=0, concat_axis=0)
+    by_heads = jnp.concatenate(k_now, axis=0)
     head_width = value_up.shape[1] // local_heads
     up_table = value_up.reshape(value_up.shape[0], local_heads, head_width)
     per_head = jnp.einsum(

time: 160 us -> 160 us (level)
  local copies, waits for them, and re-layouts: 35.5 us -> 31.8 us
  matrix products: 22.8 us -> 24.6 us
    convert_element_type x1 -> x0, local copies, waits for them, and re-layouts: 2.79 us -> none  [attend(): return latent_out.astype(jnp.bfloat16)]
    unnamed x14, local copies, waits for them, and re-layouts: 3.52 us -> 1.44 us
    dot_general x1, matrix products: 0.41 us -> 2.28 us  [per_device(): jnp.einsum('thl,lhv->thv', by_heads, up_table, preferred_element_type=jnp...]
  transfers between devices with their start and end apart: 3 -> 3, of which waited for: 3 -> 3; matrix products, arithmetic and copies ran while one was open for 3% -> 2% of each run, Pallas kernels for 0% -> 0%
where the time goes in v1:
time: 160 us; the launch traced here: 159 us
  waiting for transfers between devices  45.7 us (29%)
  blocking collectives  39.3 us (25%)
  local copies, waits for them, and re-layouts  31.8 us (20%)
  matrix products  24.6 us (15%)
  starting transfers between devices  13.4 us (8%)
  other arithmetic  4.36 us (3%)
    all_to_all x1, blocking collectives, per_device(): lax.all_to_all(outgoing, ('dp', 'tp'), split_axis=0, concat_axis=0, tiled...  39.3 us
    all_to_all x1, waiting for transfers between devices, per_device(): lax.all_to_all(answered, ('dp', 'tp'), split_axis=0, concat_axis=0, tiled...  27.8 us
    all_to_all x1, waiting for transfers between devices, per_device(): k_now = lax.all_to_all(w2, 'tp', split_axis=0, concat_axis=0)  12.2 us
    dot_general x1, matrix products, per_device(): jnp.dot(inner_act, down_local, preferred_element_type=jnp.float32)  10.9 us
    all_to_all x1, waiting for transfers between devices, sum_at_owner(): parts = lax.all_to_all(in_blocks(shard, dim, peers), axis, 0, 0, tiled=True)  5.71 us
    dot_general x1, matrix products, per_device(): jnp.dot(per_head.reshape(hidden_in.shape[0] * lax.axis_size('tp'), local_...  5.27 us
    all_to_all x1, starting transfers between devices, per_device(): k_now = lax.all_to_all(w2, 'tp', split_axis=0, concat_axis=0)  5.14 us
    reshape x1, local copies, waits for them, and re-layouts, per_device(): flat_rows = slot_rows.reshape(-1, width)  4.95 us
  transfers between devices with their start and end apart: 3, of which 3 were waited for; matrix products, arithmetic and copies ran while one was open for 2% of the time, Pallas kernels for 0%

profile of v1, /device:TPU:1, one launch (start us, length us, event | category | flops | bytes accessed | tf_op | source)
XLA Modules:
  0.0 159.4 jit_solution(5665166618368844681)
XLA Ops:
  0.0 0.0 copy-start
  0.0 1.3 reshape.91
  1.3 0.7 iota_compare_fusion.1
  2.1 1.2 fusion.32
  3.2 0.0 copy-done
  3.2 2.1 %fusion.12 = f32[16,64,128]{2,1,0:T(8,128)S(1)} fusion(f32[16,64,128]{2,1,0:T(8,128)S(1)} %fusion.32, bf16[16,64,512]{2,1,0:T(8,128)(2,1)} %param.14, bf16[16,128,512]{2,1,0:T(8,128)(2,1)S(1)} %copy-done, pred[16,128]{1,0:T(8,128)(4,1)S(1)} %iota_compare_fusion.1), kind=kOutput, calls=%fused_computation.17 | convolution fusion | flops 134610944 | bytes 4196352 | tf_op jit(solution)/shard_map/thl,tpl->thp/dot_general | solution.py:27
  5.3 0.3 fusion.31
  5.7 2.9 %convolution_convert_fusion.1 = bf16[16,64,512]{2,1,0:T(8,128)(2,1)} fusion(bf16[16,128,512]{2,1,0:T(8,128)(2,1)S(1)} %copy-done, f32[16,64]{1,0:T(8,128)S(1)} %fusion.31, f32[16,64,128]{2,1,0:T(8,128)S(1)} %fusion.12), kind=kOutput, calls=%fused_computation.12 | convolution fusion | flops 135136384 | bytes 3674112 | tf_op jit(solution)/shard_map/thp,tpl->thl/dot_general | solution.py:39
  8.6 1.3 slice_bitcast_fusion.3
  9.8 0.0 copy-start.1
  9.9 1.1 pad_maximum_fusion
  11.0 0.0 copy-start.3
  11.0 5.1 %all-to-all-start = ((bf16[4,16,16,512]{3,2,1,0:T(8,128)(2,1)}), bf16[4,16,16,512]{3,2,1,0:T(8,128)(2,1)}, u32[]{:S(2)}, u32[]{:S(2)}) async-start(bf16[4,16,16,512]{3,2,1,0:T(8,128)(2,1)} %pad_maximum_fusion), calls=%async_computation | async-start | bytes 2097152 | tf_op jit(solution)/shard_map/all_to_all | solution.py:66
  16.1 0.0 copy-done.1
  16.1 1.3 copy.19
  17.4 0.0 copy-done.3
  17.4 0.1 copy.23
  17.5 0.1 eq.15
  17.6 0.1 copy.22
  17.7 0.1 mul.71
  17.8 0.1 fusion.25
  17.9 0.2 reduce_window_sum.11
  18.0 0.2 select_reduce_fusion
  18.2 12.2 %all-to-all-done = bf16[4,16,16,512]{3,2,1,0:T(8,128)(2,1)} async-done(((bf16[4,16,16,512]{3,2,1,0:T(8,128)(2,1)}), bf16[4,16,16,512]{3,2,1,0:T(8,128)(2,1)}, u32[]{:S(2)}, u32[]{:S(2)}) %all-to-all-start) | async-done | bytes 1048608 | tf_op jit(solution)/shard_map/all_to_all | solution.py:66
  30.5 2.3 %fusion.13 = bf16[64,16,64]{2,0,1:T(8,128)(2,1)S(1)} fusion(bf16[512,16,64]{0,2,1:T(8,128)(2,1)} %bitcast.45, bf16[64,16,512]{2,1,0:T(8,128)(2,1)} %bitcast.4), kind=kOutput, calls=%fused_computation.19 | convolution fusion | flops 67174400 | bytes 2228224 | tf_op jit(solution)/shard_map/thl,lhv->thv/dot_general | solution.py:70
  32.7 0.2 copy.21
  32.9 0.2 reshape.94
  33.1 0.0 copy-start.2
  33.1 0.0 copy-start.5
  33.1 5.3 %convolution_convert_fusion = bf16[64,3584]{1,0:T(8,128)(2,1)} fusion(bf16[64,1024]{1,0:T(8,128)(2,1)S(1)} %reshape.94, bf16[1024,3584]{1,0:T(8,128)(2,1)} %param.20), kind=kOutput, calls=%fused_computation.9 | convolution fusion | flops 469991424 | bytes 7929856 | tf_op jit(solution)/shard_map/dot_general | solution.py:74
  38.4 3.5 %all-to-all-start.1 = ((bf16[4,16,3584]{2,1,0:T(8,128)(2,1)}), bf16[4,16,3584]{2,1,0:T(8,128)(2,1)S(1)}, u32[]{:S(2)}, u32[]{:S(2)}) async-start(bf16[4,16,3584]{2,1,0:T(8,128)(2,1)} %bitcast.7), calls=%async_computation.1 | async-start | bytes 917504 | tf_op jit(solution)/shard_map/all_to_all | solution.py:18
  41.9 1.0 scatter_custom_fusion
  42.9 5.7 %all-to-all-done.1 = bf16[4,16,3584]{2,1,0:T(8,128)(2,1)S(1)} async-done(((bf16[4,16,3584]{2,1,0:T(8,128)(2,1)}), bf16[4,16,3584]{2,1,0:T(8,128)(2,1)S(1)}, u32[]{:S(2)}, u32[]{:S(2)}) %all-to-all-start.1) | async-done | bytes 458784 | tf_op jit(solution)/shard_map/all_to_all | solution.py:18
  48.6 0.1 convert_reduce_fusion
  48.7 0.0 copy-done.2
  48.7 0.2 fusion.21
  48.9 0.0 copy-done.5
  48.9 0.1 fusion.23
  49.0 2.9 %gather_fusion = bf16[256,3584]{1,0:T(8,128)(2,1)} fusion(bf16[17,3584]{1,0:T(8,128)(2,1)S(1)} %concatenate.3, s32[1024]{0:T(1024)S(1)} %pad_clamp_fusion.1), kind=kCustom, calls=%fused_computation | custom fusion | bytes 3671040 | tf_op jit(solution)/shard_map/gather | solution.py:99
  51.9 4.8 %reshape.96 = bf16[128,2,3584]{2,1,0:T(2,128)(2,1)} reshape(bf16[256,3584]{1,0:T(8,128)(2,1)} %gather_fusion) | data formatting | bytes 3670016 | tf_op jit(solution)/shard_map/reshape | solution.py:99
  56.7 39.3 %all_to_all.20 = bf16[128,2,3584]{2,1,0:T(2,128)(2,1)} all-to-all(bf16[128,2,3584]{2,1,0:T(2,128)(2,1)} %reshape.96), channel_id=1, replica_groups=mesh['dp'=32,'tp'=4] {'dp','tp'}, dimensions={0} | all-to-all | bytes 3670016 | tf_op jit(solution)/shard_map/all_to_all | solution.py:102
  96.0 5.0 %reshape.97 = bf16[256,3584]{1,0:T(8,128)(2,1)} reshape(bf16[128,2,3584]{2,1,0:T(2,128)(2,1)} %all_to_all.20) | data formatting | bytes 3670016 | tf_op jit(solution)/shard_map/reshape | solution.py:104
  101.0 10.9 %fusion.5 = bf16[256,3584]{1,0:T(8,128)(2,1)} fusion(bf16[1,1024,3584]{2,1,0:T(8,128)(2,1)} %param.23, bf16[256,3584]{1,0:T(8,128)(2,1)} %reshape.97, bf16[1,3584,1024]{2,1,0:T(8,128)(2,1)} %param.22), kind=kOutput, calls=%fused_computation.8 | convolution fusion | flops 3760324608 | bytes 18350080 | tf_op jit(solution)/shard_map/dot_general | solution.py:108
  111.8 4.8 %reshape.98 = bf16[128,2,3584]{2,1,0:T(2,128)(2,1)} reshape(bf16[256,3584]{1,0:T(8,128)(2,1)} %fusion.5) | data formatting | bytes 3670016 | tf_op jit(solution)/shard_map/reshape | solution.py:109
  116.6 0.0 copy-start.4
  116.6 4.8 %all-to-all-start.3 = ((bf16[128,2,3584]{2,1,0:T(2,128)(2,1)}), bf16[128,2,3584]{2,1,0:T(2,128)(2,1)}, u32[]{:S(2)}, u32[]{:S(2)}) async-start(bf16[128,2,3584]{2,1,0:T(2,128)(2,1)} %reshape.98), calls=%async_computation.3 | async-start | bytes 3670016 | tf_op jit(solution)/shard_map/all_to_all | solution.py:110
  121.4 0.0 copy-done.4
  121.4 0.1 copy.24
  121.5 27.8 %all-to-all-done.3 = bf16[128,2,3584]{2,1,0:T(2,128)(2,1)} async-done(((bf16[128,2,3584]{2,1,0:T(2,128)(2,1)}), bf16[128,2,3584]{2,1,0:T(2,128)(2,1)}, u32[]{:S(2)}, u32[]{:S(2)}) %all-to-all-start.3) | async-done | bytes 1835040 | tf_op jit(solution)/shard_map/all_to_all | solution.py:110
  149.3 4.9 %reshape.99 = bf16[256,3584]{1,0:T(8,128)(2,1)} reshape(bf16[128,2,3584]{2,1,0:T(2,128)(2,1)} %all-to-all-done.3) | data formatting | bytes 3670016 | tf_op jit(solution)/shard_map/reshape | solution.py:111
  154.2 3.8 %gather_fusion.1 = bf16[128,3584]{1,0:T(8,128)(2,1)S(1)} fusion(bf16[256,3584]{1,0:T(8,128)(2,1)} %reshape.99, s32[1024]{0:T(1024)S(1)} %pad_clamp_fusion), kind=kCustom, calls=%fused_computation.1 | custom fusion | bytes 1835520 | tf_op jit(solution)/shard_map/gather | solution.py:112
  158.0 0.7 fusion.8
  158.7 0.7 fusion.24
  (10 shorter events, 0.1 us)
Async XLA Ops:
  0.0 3.2 %copy-start = (bf16[16,128,512]{2,1,0:T(8,128)(2,1)S(1)}, bf16[16,128,512]{2,1,0:T(8,128)(2,1)}, u32[]{:S(2)}) copy-start(bf16[16,128,512]{2,1,0:T(8,128)(2,1)} %param.16) | copy-start | bytes 6291460
  9.8 6.3 %copy-start.1 = (bf16[512,1024]{1,0:T(8,128)(2,1)S(1)}, bf16[512,1024]{1,0:T(8,128)(2,1)}, u32[]{:S(2)}) copy-start(bf16[512,1024]{1,0:T(8,128)(2,1)} %param.19) | copy-start | bytes 3145732
  11.0 6.5 %copy-start.3 = (s32[16,8]{0,1:T(8,128)S(1)}, s32[16,8]{0,1:T(8,128)}, u32[]{:S(2)}) copy-start(s32[16,8]{0,1:T(8,128)} %param.24) | copy-start | bytes 1540
  11.0 19.5 %all-to-all-start = ((bf16[4,16,16,512]{3,2,1,0:T(8,128)(2,1)}), bf16[4,16,16,512]{3,2,1,0:T(8,128)(2,1)}, u32[]{:S(2)}, u32[]{:S(2)}) async-start(bf16[4,16,16,512]{3,2,1,0:T(8,128)(2,1)} %pad_maximum_fusion), calls=%async_computation | async-start | bytes 2097152 | tf_op jit(solution)/shard_map/all_to_all | solution.py:66
  33.1 15.6 %copy-start.2 = (bf16[16,3584]{1,0:T(8,128)(2,1)S(1)}, bf16[16,3584]{1,0:T(8,128)(2,1)}, u32[]{:S(2)}) copy-start(bf16[16,3584]{1,0:T(8,128)(2,1)} %param.13) | copy-start | bytes 344068
  33.1 15.7 %copy-start.5 = (f32[3584]{0:T(1024)S(1)}, f32[3584]{0:T(1024)}, u32[]{:S(2)}) copy-start(f32[3584]{0:T(1024)} %param.21) | copy-start | bytes 43012
  38.4 10.2 %all-to-all-start.1 = ((bf16[4,16,3584]{2,1,0:T(8,128)(2,1)}), bf16[4,16,3584]{2,1,0:T(8,128)(2,1)S(1)}, u32[]{:S(2)}, u32[]{:S(2)}) async-start(bf16[4,16,3584]{2,1,0:T(8,128)(2,1)} %bitcast.7), calls=%async_computation.1 | async-start | bytes 917504 | tf_op jit(solution)/shard_map/all_to_all | solution.py:18
  116.6 4.8 %copy-start.4 = (f32[16,8]{0,1:T(8,128)S(1)}, f32[16,8]{0,1:T(8,128)}, u32[]{:S(2)}) copy-start(f32[16,8]{0,1:T(8,128)} %param.25) | copy-start | bytes 1540
  116.6 32.7 %all-to-all-start.3 = ((bf16[128,2,3584]{2,1,0:T(2,128)(2,1)}), bf16[128,2,3584]{2,1,0:T(2,128)(2,1)}, u32[]{:S(2)}, u32[]{:S(2)}) async-start(bf16[128,2,3584]{2,1,0:T(2,128)(2,1)} %reshape.98), calls=%async_computation.3 | async-start | bytes 3670016 | tf_op jit(solution)/shard_map/all_to_all | solution.py:110
